TPU v7x, 256 devices: a 2x2x32 block of a 4x8x32 slice. The times are simulated.
256 devices in a mesh: cuts: 4 (over x, y), ma: 32 (over z), mb: 2 (over core).
Axes of the slice: x: 2, y: 2, z: 32, core: 2. Of those that a mesh axis runs over, the one named last changes fastest.
The devices are a block of a 4x8x32 slice.
Arguments:
- stem_field: bfloat16 [512, 512, 2, 512], P(('cuts', 'ma', 'mb')), parts along dimension 0, may hold values from -6 to 6
- first_branch_tensors: bfloat16 [2, 2, 512, 512], P(None, None, 'ma'), may hold values from -0.1875 to 0.1875
- second_branch_tensors: bfloat16 [2, 2, 512, 512], P(None, None, 'ma'), may hold values from -0.1875 to 0.1875
- relabel: int32 [2, 512], replicated, may hold values from 0 to 511, each once within a row
- sample_block: int32 [65536, 1], P(('cuts', 'ma', 'mb')), parts along dimension 0, may hold values from 0 to 127; in each aligned block of 256 rows (0 to 255, 256 to 511, ...) at most 4 rows name the same one
- sample_state: bfloat16 [65536, 2, 512], P(('cuts', 'ma', 'mb')), parts along dimension 0, may hold values from -0.1875 to 0.1875
Outputs:
- amplitudes: bfloat16 [65536, 2, 512], P(('cuts', 'ma', 'mb')), parts along dimension 0
There are 4 independent parts, one for each index of `cuts`. A program takes and returns all parts, laid end to end along the dimension named above; an argument that names none is the same for every part. Nothing has to cross between parts.
Inputs may be any that keep to these rules, and one draw needn't show every extreme that they name: `relabel`: each row is a permutation of 0 to 511. `sample_block`: within the 256 rows of one device no prefix block is named more than 4 times.
All inputs are finite; a program needn't handle non-finite values.
Results may differ from a plain program's by a relative error of at most 0.0075.
Values may be sent and summed in bfloat16 or wider, within the bound.
A program may use at most 64 MiB of HBM per device.

v0:
```python
import jax
import jax.numpy as jnp
from jax import lax
from jax.sharding import PartitionSpec as P


def in_one_piece(arrays, axis, dim, along):
    both = jnp.concatenate(arrays, axis=along)
    filled, at, finished = (lax.all_gather(both, axis, axis=dim, tiled=True), 0, [])
    for a in arrays:
        finished.append(lax.slice_in_dim(filled, at, at + a.shape[along], axis=along))
        at += a.shape[along]
    return tuple(finished)


def complex_table(matrix):
    real_part = matrix[0]
    imag_part = matrix[1]
    upper_rows = jnp.stack([real_part, imag_part], axis=1)
    lower_rows = jnp.stack([-imag_part, real_part], axis=1)
    return jnp.stack([upper_rows, lower_rows], axis=0)


def regroup(stem_field):
    blocks, row_count, part_count, col_count = stem_field.shape
    first_count = lax.axis_size("ma")
    second_count = lax.axis_size("mb")
    groups = first_count * second_count
    pieces = stem_field.reshape(blocks, groups, row_count // groups, part_count, col_count)
    swapped_modes = lax.all_to_all(pieces, ("ma", "mb"), split_axis=1, concat_axis=1, tiled=True)
    return swapped_modes.reshape(blocks, row_count, part_count, col_count)


def on_device(
    stem_field, first_branch_tensors, second_branch_tensors, relabel, sample_block, sample_state
):
    rounds = first_branch_tensors.shape[0]
    width_first = first_branch_tensors.shape[3]
    every_first, every_second = in_one_piece(
        (first_branch_tensors, second_branch_tensors), "ma", 2, 0
    )
    positions = jnp.arange(width_first, dtype=jnp.int32)
    for regroup_round_index in range(rounds):
        stem_field = regroup(stem_field)
        first_matrix = every_first[regroup_round_index]
        second_matrix = every_second[regroup_round_index]
        selector = (relabel[regroup_round_index][:, None] == positions[None, :]).astype(
            jnp.bfloat16
        )
        permuted = jnp.einsum(
            "ij,pio->pjo", selector, first_matrix, preferred_element_type=jnp.float32
        ).astype(jnp.bfloat16)
        stem_field = jnp.einsum(
            "sapb,paqo->soqb",
            stem_field,
            complex_table(permuted),
            preferred_element_type=jnp.float32,
        ).astype(jnp.bfloat16)
        stem_field = jnp.einsum(
            "sapb,pbqo->saqo",
            stem_field,
            complex_table(second_matrix),
            preferred_element_type=jnp.float32,
        ).astype(jnp.bfloat16)
    local_blocks = stem_field.shape[0]
    groups = lax.axis_size("ma") * lax.axis_size("mb")
    block_count = local_blocks * groups
    samples = sample_state.shape[0]
    slot_bound = max(2, 2 * samples // block_count)
    state_width = sample_state.shape[2]
    owner_block = sample_block[:, 0]
    block_hot = (owner_block[:, None] == jnp.arange(block_count, dtype=jnp.int32)[None, :]).astype(
        jnp.bfloat16
    )
    order_index = jnp.arange(samples, dtype=jnp.int32)
    earlier_mask = (order_index[:, None] > order_index[None, :]).astype(jnp.bfloat16)
    earlier = jnp.dot(earlier_mask, block_hot, preferred_element_type=jnp.float32)
    slot_index = jnp.sum(earlier * block_hot.astype(jnp.float32), axis=1)
    slot_hot = (slot_index[:, None] == jnp.arange(slot_bound, dtype=jnp.float32)[None, :]).astype(
        jnp.bfloat16
    )
    dispatch = (block_hot[:, :, None] * slot_hot[:, None, :]).reshape(
        samples, block_count * slot_bound
    )
    outgoing = jnp.einsum(
        "nk,nc->kc",
        dispatch,
        sample_state.reshape(samples, 2 * state_width),
        preferred_element_type=jnp.float32,
    ).astype(jnp.bfloat16)
    outgoing = outgoing.reshape(groups, local_blocks, slot_bound, 2, state_width)
    block_table = jax.vmap(complex_table)(jnp.transpose(stem_field, (0, 2, 3, 1)))
    result = jnp.einsum(
        "gsmpb,spbqa->gsmqa",
        lax.all_to_all(outgoing, ("ma", "mb"), split_axis=0, concat_axis=0, tiled=True),
        block_table,
        preferred_element_type=jnp.float32,
    ).astype(jnp.bfloat16)
    returned = lax.all_to_all(result, ("ma", "mb"), split_axis=0, concat_axis=0, tiled=True)
    width_out = returned.shape[4]
    gathered_rows = returned.reshape(block_count * slot_bound, 2 * width_out)
    amplitudes = jnp.dot(dispatch, gathered_rows, preferred_element_type=jnp.float32).astype(
        jnp.bfloat16
    )
    return amplitudes.reshape(samples, 2, width_out)


def solution(mesh):
    placed = (
        P(("cuts", "ma", "mb"), None, None, None),
        P(None, None, "ma", None),
        P(None, None, "ma", None),
        P(),
        P(("cuts", "ma", "mb"), None),
        P(("cuts", "ma", "mb"), None, None),
    )
    return jax.shard_map(
        on_device,
        mesh=mesh,
        in_specs=placed,
        out_specs=P(("cuts", "ma", "mb"), None, None),
        check_vma=False,
    )
```

profile of v0, /device:TPU:44, one launch (start us, length us, event | category | flops | bytes accessed | tf_op | source)
XLA Modules:
  0.0 811.2 jit_solution(13682362382714095171)
XLA Ops:
  6.5 5.8 copy.46
  12.4 34.4 %all-to-all-start = ((bf16[2,64,8,2,512]{4,3,2,0,1:T(2,128)(2,1)}), bf16[2,64,8,2,512]{4,3,2,0,1:T(2,128)(2,1)}, u32[]{:S(2)}, u32[]{:S(2)}) async-start(bf16[2,64,8,2,512]{4,3,2,0,1:T(2,128)(2,1)} %copy.46), calls=%async_computation | async-start | bytes 4194304 | tf_op jit(solution)/shard_map/all_to_all | solution.py:30
  46.8 0.2 all-gather.2.cloned.1.call-start
  47.0 0.0 copy-done.6
  47.0 0.8 copy.42
  47.8 0.1 all-gather.2.cloned.1.call-update
  47.9 266.3 %all-gather.2.cloned.1.call-done = bf16[4,2,512,512]{3,0,1,2:T(4,128)(2,1)} async-done(((bf16[4,2,16,512]{3,0,1,2:T(4,128)(2,1)}), bf16[4,2,512,512]{3,0,1,2:T(4,128)(2,1)}) %all-gather.2.cloned.1.call-update) | async-done | bytes 4194320 | tf_op jit(solution)/shard_map/all_gather | solution.py:9
  314.2 7.7 fusion.65
  321.9 4.6 copy.81
  326.4 6.7 fusion.66
  333.2 1.1 copy_bitcast_fusion.1
  334.3 1.1 fusion.63
  335.4 1.5 maximum_bitcast_fusion.15
  336.9 0.8 fusion.25
  337.8 0.1 slice_bitcast_fusion.2
  337.9 1.6 maximum_bitcast_fusion.13
  339.5 0.0 all-to-all-done
  339.5 8.3 %fusion.16 = bf16[2,64,8,2,512]{4,2,1,3,0:T(8,128)(2,1)} fusion(bf16[1,512,2,512]{3,1,0,2:T(8,128)(2,1)} %get-tuple-element.26, bf16[1,512,2,512]{3,1,0,2:T(8,128)(2,1)S(1)} %copy-done.2, bf16[2,64,8,2,512]{4,3,2,0,1:T(2,128)(2,1)} %all-to-all-done, bf16[1,512,2,512]{1,3,2,0:T(8,128)(2,1)} %get-tuple-element.24, bf16[1,512,2,512]{1,3,2,0:T(8,128)(2,1)} %get-tuple-element.23), kind=kOutput, calls=%fused_computation.28 | convolution fusion | flops 4302307328 | bytes 8388608 | tf_op jit(solution)/shard_map/sapb,pbqo->saqo/dot_general | solution.py:59
  347.8 3.2 copy.52
  351.0 14.9 %all-to-all-start.1 = ((bf16[2,64,8,2,512]{4,2,3,0,1:T(8,128)(2,1)}), bf16[2,64,8,2,512]{4,2,3,0,1:T(8,128)(2,1)}, u32[]{:S(2)}, u32[]{:S(2)}) async-start(bf16[2,64,8,2,512]{4,2,3,0,1:T(8,128)(2,1)} %copy.52), calls=%async_computation.1 | async-start | bytes 4194304 | tf_op jit(solution)/shard_map/all_to_all | solution.py:30
  366.0 0.2 fusion.29
  366.2 0.1 broadcast_multiply_fusion
  366.4 0.1 mul.34
  366.5 0.1 copy.87
  366.5 0.4 convolution_convert_fusion
  367.0 1.6 reshape.149
  368.6 196.5 %all-to-all-done.1 = bf16[2,64,8,2,512]{4,2,3,0,1:T(8,128)(2,1)} async-done(((bf16[2,64,8,2,512]{4,2,3,0,1:T(8,128)(2,1)}), bf16[2,64,8,2,512]{4,2,3,0,1:T(8,128)(2,1)}, u32[]{:S(2)}, u32[]{:S(2)}) %all-to-all-start.1) | async-done | bytes 2097184 | tf_op jit(solution)/shard_map/all_to_all | solution.py:30
  565.1 7.4 all-to-all-start.2
  572.5 0.0 copy-start.1
  572.5 4.2 copy.80
  576.7 2.6 maximum_bitcast_fusion.17
  579.3 0.0 copy-done.4
  579.3 0.8 fusion.24
  580.2 0.1 slice_bitcast_fusion.4
  580.3 1.6 maximum_bitcast_fusion.11
  581.8 0.0 copy-done.3
  581.8 7.0 fusion.19
  588.8 0.1 fusion.62
  588.9 0.1 slice_bitcast_fusion
  589.1 1.7 maximum_bitcast_fusion.5
  590.8 91.0 %all-to-all-done.2 = bf16[64,2,4,2,512]{4,3,2,1,0:T(2,128)(2,1)} async-done(((bf16[64,2,4,2,512]{4,3,2,1,0:T(2,128)(2,1)}), bf16[64,2,4,2,512]{4,3,2,1,0:T(2,128)(2,1)}, u32[]{:S(2)}, u32[]{:S(2)}) %all-to-all-start.2) | async-done | bytes 1048608 | tf_op jit(solution)/shard_map/all_to_all | solution.py:95
  681.8 3.8 fusion.26
  685.6 0.8 copy.61
  686.4 114.9 %all_to_all.20 = bf16[64,2,4,2,512]{4,2,3,1,0:T(4,128)(2,1)S(1)} all-to-all(bf16[64,2,4,2,512]{4,2,3,1,0:T(4,128)(2,1)S(1)} %copy.61), channel_id=1, replica_groups=mesh['cuts'=4,'ma'=32,'mb'=2] {'ma','mb'}, dimensions={0} | all-to-all | bytes 2097152 | tf_op jit(solution)/shard_map/all_to_all | solution.py:99
  801.3 1.2 copy.62
  802.5 0.2 copy.88
  802.7 0.5 convolution_convert_fusion.3
  803.2 1.2 reshape.151
  (22 shorter events, 0.2 us)
Async XLA Ops:
  12.3 34.7 %copy-start.6 = (bf16[2,2,16,512]{3,2,1,0:T(8,128)(2,1)S(1)}, bf16[2,2,16,512]{3,2,1,0:T(8,128)(2,1)}, u32[]{:S(2)}) copy-start(bf16[2,2,16,512]{3,2,1,0:T(8,128)(2,1)} %param.8) | copy-start | bytes 196612
  12.3 34.7 %copy-start.7 = (bf16[2,2,16,512]{3,2,1,0:T(8,128)(2,1)S(1)}, bf16[2,2,16,512]{3,2,1,0:T(8,128)(2,1)}, u32[]{:S(2)}) copy-start(bf16[2,2,16,512]{3,2,1,0:T(8,128)(2,1)} %param.7) | copy-start | bytes 196612
  12.4 35.5 %copy-start.8 = (s32[2,512]{1,0:T(2,128)S(1)}, s32[2,512]{1,0:T(2,128)}, u32[]{:S(2)}) copy-start(s32[2,512]{1,0:T(2,128)} %param.9) | copy-start | bytes 12292
  12.4 327.1 %all-to-all-start = ((bf16[2,64,8,2,512]{4,3,2,0,1:T(2,128)(2,1)}), bf16[2,64,8,2,512]{4,3,2,0,1:T(2,128)(2,1)}, u32[]{:S(2)}, u32[]{:S(2)}) async-start(bf16[2,64,8,2,512]{4,3,2,0,1:T(2,128)(2,1)} %copy.46), calls=%async_computation | async-start | bytes 4194304 | tf_op jit(solution)/shard_map/all_to_all | solution.py:30
  46.8 267.5 %all-gather.2.cloned.1.call-start = ((), (), s32[]{:S(2)}) async-start(), calls=%async_computation.4 | async-start | bytes 4325376 | tf_op jit(solution)/shard_map/all_gather | solution.py:9
  337.9 1.6 copy-start.2
  351.0 14.9 %copy-start.9 = (s32[256,1]{0,1:T(1,128)S(1)}, s32[256,1]{0,1:T(1,128)}, u32[]{:S(2)}) copy-start(s32[256,1]{0,1:T(1,128)} %param.10) | copy-start | bytes 3076
  351.0 15.4 %copy-start.5 = (bf16[256,2,512]{2,1,0:T(2,128)(2,1)S(1)}, bf16[256,2,512]{2,1,0:T(2,128)(2,1)}, u32[]{:S(2)}) copy-start(bf16[256,2,512]{2,1,0:T(2,128)(2,1)} %param.11) | copy-start | bytes 1572868
  351.0 214.0 %all-to-all-start.1 = ((bf16[2,64,8,2,512]{4,2,3,0,1:T(8,128)(2,1)}), bf16[2,64,8,2,512]{4,2,3,0,1:T(8,128)(2,1)}, u32[]{:S(2)}, u32[]{:S(2)}) async-start(bf16[2,64,8,2,512]{4,2,3,0,1:T(8,128)(2,1)} %copy.52), calls=%async_computation.1 | async-start | bytes 4194304 | tf_op jit(solution)/shard_map/all_to_all | solution.py:30
  565.1 116.7 %all-to-all-start.2 = ((bf16[64,2,4,2,512]{4,3,2,1,0:T(2,128)(2,1)}), bf16[64,2,4,2,512]{4,3,2,1,0:T(2,128)(2,1)}, u32[]{:S(2)}, u32[]{:S(2)}) async-start(bf16[64,2,4,2,512]{4,3,2,1,0:T(2,128)(2,1)} %reshape.149), calls=%async_computation.2 | async-start | bytes 2097152 | tf_op jit(solution)/shard_map/all_to_all | solution.py:95
  572.4 4.2 copy-start
  572.5 4.2 copy-start.1
  576.7 2.6 copy-start.4
  580.2 1.6 copy-start.3
Sparse Core Ops, SparseCore 0:
  49.4 264.7 all-gather.1
where the time goes:
time: 812 us; the launch traced here: 811 us
  waiting for transfers between devices  554 us (68%)
  blocking collectives  115 us (14%)
  starting transfers between devices  56.9 us (7%)
  local copies, waits for them, and re-layouts  39.4 us (5%)
  matrix products  21.9 us (3%)
  between operations  13.7 us (2%)
  other arithmetic  10.5 us (1%)
    all_gather x1, waiting for transfers between devices, in_one_piece(): lax.all_gather(both, axis, axis=dim, tiled=True)  266 us
    all_to_all x2, waiting for transfers between devices, regroup(): lax.all_to_all(pieces, ('ma', 'mb'), split_axis=1, concat_axis=1, tiled=T...  196 us
    all_to_all x1, blocking collectives, on_device(): lax.all_to_all(result, ('ma', 'mb'), split_axis=0, concat_axis=0, tiled=T...  115 us
    all_to_all x1, waiting for transfers between devices, on_device(): lax.all_to_all(outgoing, ('ma', 'mb'), split_axis=0, concat_axis=0, tiled...  91 us
    all_to_all x2, starting transfers between devices, regroup(): lax.all_to_all(pieces, ('ma', 'mb'), split_axis=1, concat_axis=1, tiled=T...  49.3 us
  transfers between devices with their start and end apart: 4, of which 3 were waited for; matrix products, arithmetic and copies ran while one was open for 6% of the time, Pallas kernels for 0%

commit v1 on v0

v1 whole, which is shorter than its diff:
```python
import functools

import jax
import jax.numpy as jnp
from jax import lax
from jax.experimental import pallas as pl
from jax.experimental.pallas import tpu as pltpu
from jax.sharding import PartitionSpec as P

LANES = 128
TILE = 16
MESH = pl.DeviceIdType.MESH


def complex_table(matrix):
    real_part, imag_part = matrix[0], matrix[1]
    upper_rows = jnp.stack([real_part, imag_part], axis=1)
    lower_rows = jnp.stack([-imag_part, real_part], axis=1)
    rows, width = real_part.shape
    return jnp.stack([upper_rows, lower_rows], axis=0).reshape(2 * rows, 2 * width)


def ring_kernel(
    ring,
    mode_rows,
    kept_from,
    states_ref,
    stem_ref,
    table_ref,
    out_ref,
    states,
    sums,
    kept,
    stems,
    wide,
    products,
    coef,
    local_sem,
    stem_sem,
    state_send,
    state_recv,
    sum_send,
    sum_recv,
):
    me = lax.axis_index("ma")
    core = lax.axis_index("mb")
    right, left = lax.rem(me + 1, ring), lax.rem(me + ring - 1, ring)
    other_core = 1 - core
    last = ring

    barrier = pltpu.get_barrier_semaphore()
    pl.semaphore_signal(barrier, inc=1, device_id={"ma": right}, device_id_type=MESH)
    pl.semaphore_signal(barrier, inc=1, device_id={"ma": left}, device_id_type=MESH)
    pl.semaphore_signal(barrier, inc=1, device_id={"mb": other_core}, device_id_type=MESH)

    own_states = [
        pltpu.make_async_copy(
            states_ref.at[d if j == 0 else 1 - d], states.at[j, d], local_sem.at[2 * j + d]
        )
        for j in range(2)
        for d in range(2)
    ]
    own_stem = pltpu.make_async_copy(stem_ref, stems.at[0], local_sem.at[4])
    for copy in own_states:
        copy.start()
    own_stem.start()
    pl.semaphore_wait(barrier, 3)
    swap = pltpu.make_async_remote_copy(
        src_ref=stem_ref,
        dst_ref=stems.at[1],
        send_sem=stem_sem.at[0],
        recv_sem=stem_sem.at[1],
        device_id={"mb": other_core},
        device_id_type=MESH,
    )
    swap.start()
    for copy in own_states:
        copy.wait()

    def state_copy(d, j):
        return pltpu.make_async_remote_copy(
            src_ref=states.at[j, d],
            dst_ref=states.at[j + 2, d],
            send_sem=state_send.at[j, d],
            recv_sem=state_recv.at[j, d],
            device_id={"ma": (right, left)[d]},
            device_id_type=MESH,
        )

    def sum_copy(d, j):
        return pltpu.make_async_remote_copy(
            src_ref=sums.at[j, d],
            dst_ref=sums.at[j - 2, d],
            send_sem=sum_send.at[j - 2, d],
            recv_sem=sum_recv.at[j - 2, d],
            device_id={"ma": (left, right)[d]},
            device_id_type=MESH,
        )

    tiles = stems.shape[1]
    depth = stems.shape[3]
    half = depth // 2
    blocks = table_ref.shape[1]
    parity_row = 4 * mode_rows * mode_rows
    out_half = tiles * mode_rows * TILE

    def contribution(j, slot):
        def one(d, carry):
            real_part = states[j, d, 0:half, :]
            imag_part = states[j, d, half:depth, :]
            wide[0:half, 0:LANES] = real_part
            wide[0:half, LANES : 2 * LANES] = imag_part
            wide[half:depth, 0:LANES] = -imag_part
            wide[half:depth, LANES : 2 * LANES] = real_part
            named = states[j, d, depth : depth + TILE, :].astype(jnp.float32)[0:1, :]
            counted = lax.broadcasted_iota(jnp.int32, (blocks, LANES), 0).astype(jnp.float32)
            hot = jnp.where(counted == named, 1.0, 0.0).astype(jnp.bfloat16)
            coef[...] = jnp.dot(table_ref[...], hot, preferred_element_type=jnp.float32)

            def tile_step(t, carry):
                for h in range(2):
                    products[h] = jnp.dot(
                        stems[h, t], wide[...], preferred_element_type=jnp.float32
                    )
                odd = jnp.broadcast_to(coef[parity_row : parity_row + 1, :], (TILE, LANES)) > 0.5
                sum_real = [jnp.zeros((TILE, LANES), jnp.float32)] * mode_rows
                sum_imag = [jnp.zeros((TILE, LANES), jnp.float32)] * mode_rows
                for h in range(2):
                    for r in range(mode_rows):
                        even_rows = pl.ds(r * TILE, TILE)
                        odd_rows = pl.ds((mode_rows + r) * TILE, TILE)
                        y_real = jnp.where(
                            odd, products[h, odd_rows, 0:LANES], products[h, even_rows, 0:LANES]
                        )
                        y_imag = jnp.where(
                            odd,
                            products[h, odd_rows, LANES : 2 * LANES],
                            products[h, even_rows, LANES : 2 * LANES],
                        )
                        for q in range(mode_rows):
                            row = ((h * mode_rows + r) * 2) * mode_rows + q
                            c_real = jnp.broadcast_to(coef[row : row + 1, :], (TILE, LANES))
                            row = row + mode_rows
                            c_imag = jnp.broadcast_to(coef[row : row + 1, :], (TILE, LANES))
                            sum_real[q] = sum_real[q] + (c_real * y_real - c_imag * y_imag)
                            sum_imag[q] = sum_imag[q] + (c_real * y_imag + c_imag * y_real)
                for q in range(mode_rows):
                    start = pl.multiple_of(t * (mode_rows * TILE), TILE) + q * TILE
                    kept[slot, d, pl.ds(start, TILE), :] = sum_real[q]
                    kept[slot, d, pl.ds(out_half + start, TILE), :] = sum_imag[q]
                return carry

            return lax.fori_loop(0, tiles, tile_step, carry)

        lax.fori_loop(0, 2, one, 0)

    def spread(j, carry):
        @pl.when(j >= 2)
        def _():
            for d in range(2):
                state_copy(d, j - 2).wait_recv()

        @pl.when(j <= last - 2)
        def _():
            for d in range(2):
                state_copy(d, j).start()

        @pl.when(j == kept_from)
        def _():
            own_stem.wait()
            swap.wait()

        @pl.when(j >= kept_from)
        def _():
            contribution(j, j - kept_from)

        @pl.when(j >= last - 1)
        def _():
            for d in range(2):
                sums[j, d] = kept[j - kept_from, d].astype(jnp.bfloat16)
                sum_copy(d, j).start()

        return carry

    lax.fori_loop(0, last + 1, spread, 0)
    spare = last - kept_from

    def collect(i, carry):
        j = last - 2 - i

        @pl.when(jnp.logical_and(j < kept_from, j != 1))
        def _():
            contribution(j, spare)

        for d in range(2):
            sum_copy(d, j + 2).wait_recv()

            @pl.when(jnp.logical_and(j >= 2, j < kept_from))
            def _():
                sums[j, d] = (sums[j, d].astype(jnp.float32) + kept[spare, d]).astype(jnp.bfloat16)

            @pl.when(j >= kept_from)
            def _():
                sums[j, d] = (
                    sums[j, d].astype(jnp.float32) + kept[j - kept_from, d]
                ).astype(jnp.bfloat16)

            @pl.when(j >= 2)
            def _():
                sum_copy(d, j).start()

        return carry

    lax.fori_loop(0, last - 1, collect, 0)
    for d in range(2):
        out_ref[d] = (
            sums[0, d].astype(jnp.float32) + sums[1, 1 - d].astype(jnp.float32) + kept[spare, d]
        )

    def drain(j, carry):
        for d in range(2):
            state_copy(d, j).wait_send()
            sum_copy(d, j + 2).wait_send()
        return carry

    lax.fori_loop(0, last - 1, drain, 0)


def ring_sum(states, stem, table, ring, mode_rows):
    directions, state_rows, lanes = states.shape
    tiles, stem_rows, depth = stem.shape
    out_rows = 2 * tiles * mode_rows * TILE
    slots = ring + 1
    kept_from = max(2, slots - 15)
    hops = (ring - 1, directions)
    return pl.pallas_call(
        functools.partial(ring_kernel, ring, mode_rows, kept_from),
        out_shape=jax.ShapeDtypeStruct((directions, out_rows, lanes), jnp.float32),
        in_specs=[
            pl.BlockSpec(memory_space=pl.ANY),
            pl.BlockSpec(memory_space=pl.ANY),
            pl.BlockSpec(memory_space=pltpu.VMEM),
        ],
        out_specs=pl.BlockSpec(memory_space=pltpu.VMEM),
        scratch_shapes=[
            pltpu.VMEM((slots, directions, state_rows, lanes), jnp.bfloat16),
            pltpu.VMEM((slots, directions, out_rows, lanes), jnp.bfloat16),
            pltpu.VMEM((slots - kept_from, directions, out_rows, lanes), jnp.float32),
            pltpu.VMEM((2, tiles, stem_rows, depth), jnp.bfloat16),
            pltpu.VMEM((depth, 2 * lanes), jnp.bfloat16),
            pltpu.VMEM((2, stem_rows, 2 * lanes), jnp.float32),
            pltpu.VMEM((table.shape[0], lanes), jnp.float32),
            pltpu.SemaphoreType.DMA((5,)),
            pltpu.SemaphoreType.DMA((2,)),
            pltpu.SemaphoreType.DMA(hops),
            pltpu.SemaphoreType.DMA(hops),
            pltpu.SemaphoreType.DMA(hops),
            pltpu.SemaphoreType.DMA(hops),
        ],
        compiler_params=pltpu.CompilerParams(
            collective_id=0, has_side_effects=True, vmem_limit_bytes=61 * 1024 * 1024
        ),
    )(states, stem, table)


def split(exact):
    upper = lax.reduce_precision(exact, exponent_bits=8, mantissa_bits=7)
    return upper.astype(jnp.bfloat16), (exact - upper).astype(jnp.bfloat16)


def on_device(
    stem_field, first_branch_tensors, second_branch_tensors, relabel, sample_block, sample_state
):
    ring = lax.axis_size("ma")
    groups = ring * lax.axis_size("mb")
    local_blocks, row_count, _, width = stem_field.shape
    mode_rows = row_count // groups
    tiles = groups // TILE
    depth = 2 * width
    block_count = local_blocks * groups
    samples = sample_state.shape[0]
    directions = samples // LANES
    assert lax.axis_size("mb") == 2 and local_blocks == 2 and directions == 2
    assert groups % TILE == 0 and block_count <= 256

    both = jnp.concatenate([first_branch_tensors, second_branch_tensors], axis=0)
    both = lax.all_gather(both, "ma", axis=2, tiled=True)
    rounds = first_branch_tensors.shape[0]
    every_first, every_second = both[:rounds], both[rounds:]

    core = lax.axis_index("mb")
    group = lax.axis_index("ma") * 2 + core
    partner = lax.axis_index("ma") * 2 + 1 - core

    stem = stem_field.reshape(local_blocks, tiles, TILE, mode_rows, depth)
    stem = jnp.transpose(stem, (1, 0, 3, 2, 4)).reshape(row_count * local_blocks, depth)
    inner, outer = complex_table(every_second[0]), complex_table(every_second[1])
    parts = split(jnp.dot(stem, inner, preferred_element_type=jnp.float32))
    stem = sum(jnp.dot(part, outer, preferred_element_type=jnp.float32) for part in parts)
    stem = stem.astype(jnp.bfloat16)
    stem = stem.reshape(tiles, local_blocks * mode_rows * TILE, depth)

    near = jnp.concatenate(
        [group * mode_rows + jnp.arange(mode_rows), partner * mode_rows + jnp.arange(mode_rows)]
    )
    near_hot = (relabel[0][:, None] == near[None, :]).astype(jnp.bfloat16)
    near_rows = jnp.einsum(
        "ij,pio->jpo", near_hot, every_first[0], preferred_element_type=jnp.float32
    ).astype(jnp.bfloat16)
    near_rows = near_rows.reshape(2 * mode_rows, 2, groups, mode_rows)
    table = jnp.transpose(near_rows, (0, 1, 3, 2)).reshape(4 * mode_rows * mode_rows, groups)
    table = jnp.repeat(table, local_blocks, axis=1)
    parity = (jnp.arange(block_count) % local_blocks).astype(jnp.bfloat16)
    table = jnp.concatenate([table, jnp.broadcast_to(parity, (TILE, block_count))], axis=0)

    states = jnp.transpose(sample_state.reshape(directions, LANES, depth), (0, 2, 1))
    named = sample_block.reshape(directions, 1, LANES).astype(jnp.bfloat16)
    states = jnp.concatenate(
        [states, jnp.broadcast_to(named, (directions, TILE, LANES))], axis=1
    )
    summed = ring_sum(states, stem, table, ring, mode_rows)

    order = jnp.arange(row_count).reshape(tiles, TILE, mode_rows)
    order = jnp.transpose(order, (0, 2, 1)).reshape(row_count)
    last_hot = (relabel[1][:, None] == order[None, :]).astype(jnp.bfloat16)
    last = jnp.einsum(
        "ij,pio->pjo", last_hot, every_first[1], preferred_element_type=jnp.float32
    ).astype(jnp.bfloat16)
    final = complex_table(last)
    amplitudes = sum(
        jnp.einsum("dkn,km->dnm", part, final, preferred_element_type=jnp.float32)
        for part in split(summed)
    ).astype(jnp.bfloat16)
    return amplitudes.reshape(samples, 2, last.shape[2])


def solution(mesh):
    placed = (
        P(("cuts", "ma", "mb"), None, None, None),
        P(None, None, "ma", None),
        P(None, None, "ma", None),
        P(),
        P(("cuts", "ma", "mb"), None),
        P(("cuts", "ma", "mb"), None, None),
    )
    return jax.shard_map(
        on_device,
        mesh=mesh,
        in_specs=placed,
        out_specs=P(("cuts", "ma", "mb"), None, None),
        check_vma=False,
    )
```

time: 812 us -> 600 us (0.74)
  waiting for transfers between devices: 554 us -> 142 us
  Pallas kernels: 0 us -> 398 us
  blocking collectives: 115 us -> 0 us
  starting transfers between devices: 56.9 us -> 0.01 us
  local copies, waits for them, and re-layouts: 39.4 us -> 25 us
    pallas_call x0 -> x1, Pallas kernels: none -> 398 us  [ring_sum(): pl.pallas_call(functools.partial(ring_kernel, ring, mode_rows, kept_from)...]
    all_to_all x3 -> x0, waiting for transfers between devices: 287 us -> none  [the longest x2 196 us: regroup(): lax.all_to_all(pieces, ('ma', 'mb'), split_axis=1, concat_axis=1, tiled=T...]
    all_gather x1, waiting for transfers between devices: 266 us -> 142 us  [on_device(): both = lax.all_gather(both, 'ma', axis=2, tiled=True)]
    all_to_all x1 -> x0, blocking collectives: 115 us -> none  [on_device(): lax.all_to_all(result, ('ma', 'mb'), split_axis=0, concat_axis=0, tiled=T...]
    all_to_all x3 -> x0, starting transfers between devices: 56.7 us -> none  [the longest x2 49.3 us: regroup(): lax.all_to_all(pieces, ('ma', 'mb'), split_axis=1, concat_axis=1, tiled=T...]
    slice x3 -> x1, local copies, waits for them, and re-layouts: 14.4 us -> 0.01 us  [on_device(): near_hot = (relabel[0][:, None] == near[None, :]).astype(jnp.bfloat16)]
    another operation x0 -> x3, local copies, waits for them, and re-layouts: none -> 8.31 us  [complex_table(): jnp.stack([upper_rows, lower_rows], axis=0).reshape(2 * rows, 2 * width)]
    dot_general x8 -> x7, matrix products: 21.9 us -> 15.4 us  [the longest x2 6.63 us: on_device(): jnp.dot(part, outer, preferred_element_type=jnp.float32)]
  transfers between devices with their start and end apart: 4 -> 1, of which waited for: 3 -> 1; matrix products, arithmetic and copies ran while one was open for 6% -> 1% of each run, Pallas kernels for 0% -> 0%
where the time goes in v1:
time: 600 us
  Pallas kernels  398 us (66%)
  waiting for transfers between devices  142 us (24%)
  local copies, waits for them, and re-layouts  25 us (4%)
  matrix products  15.4 us (3%)
  between operations  13.7 us (2%)
    pallas_call x1, Pallas kernels, ring_sum(): pl.pallas_call(functools.partial(ring_kernel, ring, mode_rows, kept_from)...  398 us
    all_gather x1, waiting for transfers between devices, on_device(): both = lax.all_gather(both, 'ma', axis=2, tiled=True)  142 us
  transfers between devices with their start and end apart: 1, of which 1 were waited for; matrix products, arithmetic and copies ran while one was open for 1% of the time, Pallas kernels for 0%

profile of v1, /device:TPU:44, one launch (start us, length us, event | category | flops | bytes accessed | tf_op | source)
XLA Modules:
  0.0 599.8 jit_solution(13583177460103091514)
XLA Ops:
  6.5 0.0 all-gather.2.cloned.1.call-start
  6.6 1.5 pad_maximum_fusion.4
  8.1 0.1 all-gather.2.cloned.1.call-update
  8.2 0.1 reshape.143
  8.3 1.4 reshape.128
  9.7 0.3 copy.21
  9.9 3.2 reshape.130
  13.2 0.0 copy-start.3
  13.2 0.0 copy-start.2
  13.2 2.5 copy.23
  15.7 0.1 pad_add_fusion
  15.8 0.0 copy-done.3
  15.8 0.0 copy-done.2
  15.9 0.9 pad_maximum_fusion.3.states_ref
  16.7 142.3 %all-gather.2.cloned.1.call-done = bf16[4,2,512,512]{3,2,1,0:T(8,128)(2,1)} async-done(((bf16[4,2,16,512]{3,2,1,0:T(8,128)(2,1)}), bf16[4,2,512,512]{3,2,1,0:T(8,128)(2,1)}) %all-gather.2.cloned.1.call-update) | async-done | bytes 4194320 | tf_op jit(solution)/shard_map/all_gather | solution.py:287
  159.0 2.0 fusion.4
  161.1 0.1 slice_bitcast_fusion.4
  161.2 1.5 convolution_convert_fusion.1
  162.7 0.2 copy.25
  162.9 0.2 copy.26
  163.1 0.1 copy.27
  163.3 0.1 copy.28
  163.4 0.2 maximum_bitcast_fusion.4
  163.6 0.2 pad_maximum_fusion.2
  163.8 4.0 copy.30
  167.8 3.4 reshape.148
  171.2 1.3 fusion.18
  172.5 1.7 slice_bitcast_fusion.8
  174.2 0.4 maximum_bitcast_fusion
  174.5 0.2 pad_maximum_fusion
  174.7 2.2 copy.22
  176.9 0.6 copy.36
  177.5 0.2 pad_maximum_fusion.1
  177.7 2.2 copy.24
  179.9 0.0 copy-start.1
  179.9 0.6 copy.37
  180.4 1.0 copy-done.1
  181.4 2.4 fusion.22
  183.8 2.5 fusion.1
  186.3 4.2 add_convert_fusion
  190.5 0.6 pad_maximum_fusion.5.table_ref
  191.1 397.9 %shard_map.64 = f32[2,1024,128]{2,1,0:T(8,128)} custom-call(bf16[2,1040,128]{2,1,0:T(8,128)(2,1)} %pad_maximum_fusion.3.states_ref, bf16[4,256,1024]{2,1,0:T(8,128)(2,1)} %bitcast.81, bf16[272,128]{1,0:T(8,128)(2,1)} %pad_maximum_fusion.5.table_ref), custom_call_target="tpu_custom_call" | custom-call | tf_op jit(solution)/shard_map/pallas_call | solution.py:236
  589.0 0.0 copy-start
  589.0 2.0 fusion.10
  591.1 0.0 copy-done
  591.1 0.7 fusion.5
  591.8 1.2 reshape.145
  (10 shorter events, 0.2 us)
Async XLA Ops:
  6.5 152.5 %all-gather.2.cloned.1.call-start = ((), (), s32[]{:S(2)}) async-start(), calls=%async_computation | async-start | bytes 4325376 | tf_op jit(solution)/shard_map/all_gather | solution.py:287
  13.2 2.6 copy-start.3
  13.2 2.7 copy-start.2
  179.9 1.6 copy-start.1
  589.0 2.1 copy-start
Sparse Core Ops, SparseCore 0:
  9.2 149.8 all-gather.1

commit v2 on v1

--- a/solution.py
+++ b/solution.py
@@ -9,15 +9,167 @@
 
 LANES = 128
 TILE = 16
+PACE = 3
+KEPT = 15
 MESH = pl.DeviceIdType.MESH
 
 
 def complex_table(matrix):
     real_part, imag_part = matrix[0], matrix[1]
-    upper_rows = jnp.stack([real_part, imag_part], axis=1)
-    lower_rows = jnp.stack([-imag_part, real_part], axis=1)
-    rows, width = real_part.shape
-    return jnp.stack([upper_rows, lower_rows], axis=0).reshape(2 * rows, 2 * width)
+    upper_rows = jnp.concatenate([real_part, imag_part], axis=1)
+    lower_rows = jnp.concatenate([-imag_part, real_part], axis=1)
+    return jnp.concatenate([upper_rows, lower_rows], axis=0)
+
+
+def spread_kernel(
+    ring,
+    states_ref,
+    shard_ref,
+    states,
+    gathered,
+    local_sem,
+    pair_sem,
+    state_send,
+    state_recv,
+    shard_send,
+    shard_recv,
+):
+    me = lax.axis_index("ma")
+    core = lax.axis_index("mb")
+    right, left = lax.rem(me + 1, ring), lax.rem(me + ring - 1, ring)
+    other_core = 1 - core
+    hops = ring // 2
+    rows = shard_ref.shape[2]
+    part = shard_ref.shape[0] // 2
+
+    barrier = pltpu.get_barrier_semaphore()
+    pl.semaphore_signal(barrier, inc=1, device_id={"ma": right}, device_id_type=MESH)
+    pl.semaphore_signal(barrier, inc=1, device_id={"ma": left}, device_id_type=MESH)
+    pl.semaphore_signal(barrier, inc=1, device_id={"mb": other_core}, device_id_type=MESH)
+
+    def held(owner):
+        start = pl.multiple_of(owner * rows, rows)
+        return gathered.at[pl.ds(core * part, part), :, pl.ds(start, rows), :]
+
+    local = [
+        pltpu.make_async_copy(
+            states_ref.at[d if j == 0 else 1 - d], states.at[j, d], local_sem.at[2 * j + d]
+        )
+        for j in range(2)
+        for d in range(2)
+    ]
+    local.append(
+        pltpu.make_async_copy(
+            shard_ref.at[pl.ds(core * part, part)], held(me), local_sem.at[4]
+        )
+    )
+    for copy in local:
+        copy.start()
+    pl.semaphore_wait(barrier, 3)
+    for copy in local:
+        copy.wait()
+
+    def state_copy(d, j):
+        return pltpu.make_async_remote_copy(
+            src_ref=states.at[j, d],
+            dst_ref=states.at[j + 2, d],
+            send_sem=state_send.at[j, d],
+            recv_sem=state_recv.at[j, d],
+            device_id={"ma": (right, left)[d]},
+            device_id_type=MESH,
+        )
+
+    def shard_copy(d, i, owner):
+        return pltpu.make_async_remote_copy(
+            src_ref=held(owner),
+            dst_ref=held(owner),
+            send_sem=shard_send.at[i, d],
+            recv_sem=shard_recv.at[i, d],
+            device_id={"ma": (right, left)[d]},
+            device_id_type=MESH,
+        )
+
+    def owner_of(d, i):
+        return lax.rem(me + ring - i, ring) if d == 0 else lax.rem(me + i, ring)
+
+    def hop(i, carry):
+        for d in range(2):
+
+            @pl.when(i >= 1)
+            def _():
+                shard_copy(d, i - 1, owner_of(d, i)).wait_recv()
+
+        shard_copy(0, i, owner_of(0, i)).start()
+
+        @pl.when(i < hops - 1)
+        def _():
+            shard_copy(1, i, owner_of(1, i)).start()
+
+        for d in range(2):
+
+            @pl.when(i >= 2)
+            def _():
+                state_copy(d, i - 2).wait_recv()
+
+            state_copy(d, i).start()
+
+        return carry
+
+    lax.fori_loop(0, hops, hop, 0)
+    shard_copy(0, hops - 1, owner_of(0, hops)).wait_recv()
+    mine = gathered.at[pl.ds(core * part, part)]
+    pair = pltpu.make_async_remote_copy(
+        src_ref=mine,
+        dst_ref=mine,
+        send_sem=pair_sem.at[0],
+        recv_sem=pair_sem.at[1],
+        device_id={"mb": other_core},
+        device_id_type=MESH,
+    )
+    pair.start()
+    for d in range(2):
+        state_copy(d, hops - 2).wait_recv()
+        state_copy(d, hops - 1).wait_recv()
+
+    def drain(i, carry):
+        for d in range(2):
+            state_copy(d, i).wait_send()
+        shard_copy(0, i, owner_of(0, i)).wait_send()
+
+        @pl.when(i < hops - 1)
+        def _():
+            shard_copy(1, i, owner_of(1, i)).wait_send()
+
+        return carry
+
+    lax.fori_loop(0, hops, drain, 0)
+    pair.wait()
+
+
+def first_spread(states, shard, ring):
+    directions, state_rows, lanes = states.shape
+    tensors, parts, rows, width = shard.shape
+    hops = (ring // 2, directions)
+    return pl.pallas_call(
+        functools.partial(spread_kernel, ring),
+        out_shape=(
+            jax.ShapeDtypeStruct((ring // 2 + 2, directions, state_rows, lanes), jnp.bfloat16),
+            jax.ShapeDtypeStruct((tensors, parts, ring * rows, width), jnp.bfloat16),
+        ),
+        in_specs=[pl.BlockSpec(memory_space=pl.ANY)] * 2,
+        out_specs=(pl.BlockSpec(memory_space=pltpu.VMEM),) * 2,
+        scratch_shapes=[
+            pltpu.SemaphoreType.DMA((5,)),
+            pltpu.SemaphoreType.DMA((2,)),
+            pltpu.SemaphoreType.DMA(hops),
+            pltpu.SemaphoreType.DMA(hops),
+            pltpu.SemaphoreType.DMA(hops),
+            pltpu.SemaphoreType.DMA(hops),
+        ],
+        compiler_params=pltpu.CompilerParams(
+            collective_id=1, has_side_effects=True, vmem_limit_bytes=61 * 1024 * 1024
+        ),
+    )(states, shard)
 
 
 def ring_kernel(
@@ -53,16 +205,13 @@
     pl.semaphore_signal(barrier, inc=1, device_id={"ma": left}, device_id_type=MESH)
     pl.semaphore_signal(barrier, inc=1, device_id={"mb": other_core}, device_id_type=MESH)
 
-    own_states = [
-        pltpu.make_async_copy(
-            states_ref.at[d if j == 0 else 1 - d], states.at[j, d], local_sem.at[2 * j + d]
-        )
-        for j in range(2)
-        for d in range(2)
-    ]
-    own_stem = pltpu.make_async_copy(stem_ref, stems.at[0], local_sem.at[4])
-    for copy in own_states:
-        copy.start()
+    arrived = states_ref.shape[0]
+    first = arrived - 2
+    own_states = pltpu.make_async_copy(
+        states_ref, states.at[pl.ds(0, arrived)], local_sem.at[0]
+    )
+    own_stem = pltpu.make_async_copy(stem_ref, stems.at[0], local_sem.at[1])
+    own_states.start()
     own_stem.start()
     pl.semaphore_wait(barrier, 3)
     swap = pltpu.make_async_remote_copy(
@@ -74,15 +223,14 @@
         device_id_type=MESH,
     )
     swap.start()
-    for copy in own_states:
-        copy.wait()
+    own_states.wait()
 
     def state_copy(d, j):
         return pltpu.make_async_remote_copy(
             src_ref=states.at[j, d],
             dst_ref=states.at[j + 2, d],
-            send_sem=state_send.at[j, d],
-            recv_sem=state_recv.at[j, d],
+            send_sem=state_send.at[j - first, d],
+            recv_sem=state_recv.at[j - first, d],
             device_id={"ma": (right, left)[d]},
             device_id_type=MESH,
         )
@@ -155,7 +303,7 @@
         lax.fori_loop(0, 2, one, 0)
 
     def spread(j, carry):
-        @pl.when(j >= 2)
+        @pl.when(j >= arrived)
         def _():
             for d in range(2):
                 state_copy(d, j - 2).wait_recv()
@@ -182,22 +330,19 @@
 
         return carry
 
-    lax.fori_loop(0, last + 1, spread, 0)
-    spare = last - kept_from
+    lax.fori_loop(first, last + 1, spread, 0)
+    slots = last + 1 - kept_from
 
     def collect(i, carry):
         j = last - 2 - i
 
-        @pl.when(jnp.logical_and(j < kept_from, j != 1))
-        def _():
-            contribution(j, spare)
-
         for d in range(2):
             sum_copy(d, j + 2).wait_recv()
 
             @pl.when(jnp.logical_and(j >= 2, j < kept_from))
             def _():
-                sums[j, d] = (sums[j, d].astype(jnp.float32) + kept[spare, d]).astype(jnp.bfloat16)
+                slot = slots - 1 - lax.rem(kept_from - 1 - j, slots)
+                sums[j, d] = (sums[j, d].astype(jnp.float32) + kept[slot, d]).astype(jnp.bfloat16)
 
             @pl.when(j >= kept_from)
             def _():
@@ -209,17 +354,28 @@
             def _():
                 sum_copy(d, j).start()
 
+        turn = i - (i + 1) // PACE
+
+        @pl.when(jnp.logical_and(lax.rem(i, PACE) != PACE - 1, turn <= kept_from - 2))
+        def _():
+            contribution(kept_from - 1 - turn, slots - 1 - lax.rem(turn, slots))
+
         return carry
 
     lax.fori_loop(0, last - 1, collect, 0)
+    mine = slots - 1 - (kept_from - 2) % slots
     for d in range(2):
         out_ref[d] = (
-            sums[0, d].astype(jnp.float32) + sums[1, 1 - d].astype(jnp.float32) + kept[spare, d]
+            sums[0, d].astype(jnp.float32) + sums[1, 1 - d].astype(jnp.float32) + kept[mine, 1 - d]
         )
 
     def drain(j, carry):
         for d in range(2):
-            state_copy(d, j).wait_send()
+
+            @pl.when(j >= first)
+            def _():
+                state_copy(d, j).wait_send()
+
             sum_copy(d, j + 2).wait_send()
         return carry
 
@@ -227,12 +383,17 @@
 
 
 def ring_sum(states, stem, table, ring, mode_rows):
-    directions, state_rows, lanes = states.shape
+    arrived, directions, state_rows, lanes = states.shape
     tiles, stem_rows, depth = stem.shape
     out_rows = 2 * tiles * mode_rows * TILE
     slots = ring + 1
-    kept_from = max(2, slots - 15)
+    kept_from = max(arrived, slots - KEPT)
+    turns = kept_from - 1
+    for turn in range(turns):
+        step = (PACE * turn) // (PACE - 1)
+        assert step < min(ring - 1, ring - kept_from - 1 + turn)
     hops = (ring - 1, directions)
+    left = (ring + 1 - arrived, directions)
     return pl.pallas_call(
         functools.partial(ring_kernel, ring, mode_rows, kept_from),
         out_shape=jax.ShapeDtypeStruct((directions, out_rows, lanes), jnp.float32),
@@ -250,10 +411,10 @@
             pltpu.VMEM((depth, 2 * lanes), jnp.bfloat16),
             pltpu.VMEM((2, stem_rows, 2 * lanes), jnp.float32),
             pltpu.VMEM((table.shape[0], lanes), jnp.float32),
-            pltpu.SemaphoreType.DMA((5,)),
             pltpu.SemaphoreType.DMA((2,)),
-            pltpu.SemaphoreType.DMA(hops),
-            pltpu.SemaphoreType.DMA(hops),
+            pltpu.SemaphoreType.DMA((2,)),
+            pltpu.SemaphoreType.DMA(left),
+            pltpu.SemaphoreType.DMA(left),
             pltpu.SemaphoreType.DMA(hops),
             pltpu.SemaphoreType.DMA(hops),
         ],
@@ -284,7 +445,12 @@
     assert groups % TILE == 0 and block_count <= 256
 
     both = jnp.concatenate([first_branch_tensors, second_branch_tensors], axis=0)
-    both = lax.all_gather(both, "ma", axis=2, tiled=True)
+    states = jnp.transpose(sample_state.reshape(directions, LANES, depth), (0, 2, 1))
+    named = sample_block.reshape(directions, 1, LANES).astype(jnp.bfloat16)
+    states = jnp.concatenate(
+        [states, jnp.broadcast_to(named, (directions, TILE, LANES))], axis=1
+    )
+    states, both = first_spread(states, both, ring)
     rounds = first_branch_tensors.shape[0]
     every_first, every_second = both[:rounds], both[rounds:]
 
@@ -313,11 +479,6 @@
     parity = (jnp.arange(block_count) % local_blocks).astype(jnp.bfloat16)
     table = jnp.concatenate([table, jnp.broadcast_to(parity, (TILE, block_count))], axis=0)
 
-    states = jnp.transpose(sample_state.reshape(directions, LANES, depth), (0, 2, 1))
-    named = sample_block.reshape(directions, 1, LANES).astype(jnp.bfloat16)
-    states = jnp.concatenate(
-        [states, jnp.broadcast_to(named, (directions, TILE, LANES))], axis=1
-    )
     summed = ring_sum(states, stem, table, ring, mode_rows)
 
     order = jnp.arange(row_count).reshape(tiles, TILE, mode_rows)

time: 600 us -> 466 us (0.78)
  waiting for transfers between devices: 142 us -> 0 us
  Pallas kernels: 398 us -> 434 us
  between operations: 13.7 us -> 0.19 us
  local copies, waits for them, and re-layouts: 25 us -> 11.6 us
    pallas_call x0 -> x1, Pallas kernels: none -> 145 us  [first_spread(): pl.pallas_call(functools.partial(spread_kernel, ring), out_shape=(jax.Sha...]
    all_gather x1 -> x0, waiting for transfers between devices: 142 us -> none  [on_device(): both = lax.all_gather(both, 'ma', axis=2, tiled=True)]
    pallas_call x1, Pallas kernels: 398 us -> 289 us  [ring_sum(): pl.pallas_call(functools.partial(ring_kernel, ring, mode_rows, kept_from)...]
    another operation x5 -> x0, local copies, waits for them, and re-layouts: 10 us -> none  [the longest x3 8.31 us: complex_table(): jnp.stack([upper_rows, lower_rows], axis=0).reshape(2 * rows, 2 * width)]
  transfers between devices with their start and end apart: 1 -> 0, of which waited for: 1 -> 0; matrix products, arithmetic and copies ran while one was open for 1% -> 0% of each run, Pallas kernels for 0% -> 0%
where the time goes in v2:
time: 466 us; the launch traced here: 465 us
  Pallas kernels  434 us (93%)
  matrix products  15.4 us (3%)
  local copies, waits for them, and re-layouts  11.6 us (2%)
    pallas_call x1, Pallas kernels, ring_sum(): pl.pallas_call(functools.partial(ring_kernel, ring, mode_rows, kept_from)...  289 us
    pallas_call x1, Pallas kernels, first_spread(): pl.pallas_call(functools.partial(spread_kernel, ring), out_shape=(jax.Sha...  145 us

profile of v2, /device:TPU:44, one launch (start us, length us, event | category | flops | bytes accessed | tf_op | source)
XLA Modules:
  0.0 465.1 jit_solution(9603481194659365035)
XLA Ops:
  0.0 0.1 pad_add_fusion
  0.1 0.7 convert_reduce_fusion
  0.8 0.8 fusion.38
  1.6 0.1 reshape.100
  1.7 1.5 pad_maximum_fusion.1.shard_ref
  3.2 1.4 reshape.87
  4.6 0.3 copy.22
  4.9 0.9 pad_maximum_fusion.states_ref
  5.7 3.2 reshape.88
  9.0 2.5 copy.23
  11.5 145.1 %shard_map.64 = (bf16[18,2,1040,128]{3,2,1,0:T(8,128)(2,1)}, bf16[4,2,512,512]{3,2,1,0:T(8,128)(2,1)}) custom-call(bf16[2,1040,128]{2,1,0:T(8,128)(2,1)} %pad_maximum_fusion.states_ref, bf16[4,2,16,512]{3,2,1,0:T(8,128)(2,1)} %pad_maximum_fusion.1.shard_ref), custom_call_target="tpu_custom_call" | custom-call | tf_op jit(solution)/shard_map/pallas_call | solution.py:153
  156.6 1.5 convolution_convert_fusion.1
  158.1 0.2 copy.24
  158.3 0.2 copy.25
  158.5 0.1 copy.26
  158.7 0.1 copy.27
  158.8 0.0 copy-start
  158.8 0.6 pad_maximum_fusion.2.table_ref
  159.4 2.4 fusion.12
  161.9 0.0 copy-start.1
  161.9 0.1 slice_bitcast_fusion
  162.0 0.0 copy-done
  162.0 0.1 fusion.36
  162.1 0.1 slice_bitcast_fusion.2
  162.2 1.3 copy-done.1
  163.5 2.4 fusion.4
  165.8 2.4 fusion.1
  168.3 3.8 add_convert_fusion
  172.1 288.9 %shard_map.65 = f32[2,1024,128]{2,1,0:T(8,128)} custom-call(bf16[18,2,1040,128]{3,2,1,0:T(8,128)(2,1)} %get-tuple-element.7.states_ref, bf16[4,256,1024]{2,1,0:T(8,128)(2,1)} %bitcast.63, bf16[272,128]{1,0:T(8,128)(2,1)} %pad_maximum_fusion.2.table_ref), custom_call_target="tpu_custom_call" | custom-call | tf_op jit(solution)/shard_map/pallas_call | solution.py:397
  461.0 0.0 copy-start.2
  461.0 2.1 fusion.13
  463.1 0.0 copy-done.2
  463.1 0.8 fusion.14
  463.9 1.2 reshape.101
  (8 shorter events, 0.1 us)
Async XLA Ops:
  158.8 3.2 copy-start
  161.9 1.6 copy-start.1
  461.0 2.1 copy-start.2
